TPU v7x, 32 devices: a whole 2x2x4 slice. The times are simulated.
32 devices in a mesh: row: 8 (over z, core), col: 4 (over y, x).
Axes of the slice: x: 2, y: 2, z: 4, core: 2. Of those that a mesh axis runs over, the one named last changes fastest.
Arguments:
- loadings: bfloat16 [8, 32768, 1024], P(None, 'row', 'col'), may hold values from -6 to 6
- weights: bfloat16 [8, 32768, 512], P(None, 'row', 'col'), may hold values from -0.03125 to 0.03125
- specific: float32 [8, 32768], P(None, 'row'), may hold values from 0.2 to 5
- factor_cov: float32 [8, 1024, 1024], P(None, 'col'), may hold values from -0.001953125 to 0.0048828125, as said below
Outputs:
- portfolio_cov: float32 [8, 512, 512], P(None, 'row', 'col')
Inputs may be any that keep to these rules, and one draw needn't show every extreme that they name: `factor_cov`: each day's matrix is a symmetric positive definite factor covariance of order 1024.
All inputs are finite; a program needn't handle non-finite values.
Results may differ from a plain program's by a relative error of at most 0.0003.
Values may be sent and summed in bfloat16 or wider, within the bound.
A program may use at most 128 MiB of HBM per device.

v0:
```python
import jax
import jax.numpy as jnp
from jax import lax
from jax.sharding import PartitionSpec as P


def shards(loadings, weights, specific, factor_cov):
    factor_cols = loadings.shape[2]
    port_cols = weights.shape[2]
    total_ports = port_cols * lax.axis_size("col")
    port_rows = total_ports // lax.axis_size("row")
    row_start = lax.axis_index("row") * port_rows
    weighted = (specific[:, :, None] * weights.astype(jnp.float32)).astype(jnp.bfloat16)
    fragment = lax.all_gather(weights, "col", axis=2, tiled=True)
    exposure_part = jnp.einsum(
        "dar,dap->drp", loadings, fragment, preferred_element_type=jnp.float32
    )
    specific_term = jnp.einsum(
        "dak,dap->dkp", weighted, fragment, preferred_element_type=jnp.float32
    )
    joined = jnp.concatenate([exposure_part, specific_term], axis=1)
    exposure = lax.psum(joined[:, :factor_cols, :], "row")
    specific_block = lax.psum_scatter(
        joined[:, factor_cols:, :], "row", scatter_dimension=2, tiled=True
    )
    exposure_rows = lax.dynamic_slice_in_dim(exposure, row_start, port_rows, 2)
    left_part = jnp.einsum(
        "dri,drs->dis", exposure_rows, factor_cov, precision=lax.Precision.HIGHEST
    )
    left = lax.psum(left_part, "col")
    exposure_cols = lax.all_to_all(exposure, "col", split_axis=2, concat_axis=1, tiled=True)
    factor_block = jnp.einsum("dir,drk->dik", left, exposure_cols, precision=lax.Precision.HIGHEST)
    return factor_block + jnp.swapaxes(specific_block, 1, 2)


def solution(mesh):
    in_specs = (P(None, "row", "col"), P(None, "row", "col"), P(None, "row"), P(None, "col", None))
    out_specs = P(None, "row", "col")
    return jax.shard_map(shards, mesh=mesh, in_specs=in_specs, out_specs=out_specs, check_vma=False)
```

profile of v0, /device:TPU:0, one launch (start us, length us, event | category | flops | bytes accessed | tf_op | source)
XLA Modules:
  0.0 558.4 jit_solution(18040227865551506382)
XLA Ops:
  6.5 0.0 all-gather.2.cloned.1.call-start
  6.5 0.7 all-gather.2.cloned.1.call-update
  7.3 0.0 copy-start
  7.3 0.0 all-reduce.3.cloned.1.call-start
  7.3 301.6 %all-gather.2.cloned.1.call-done = bf16[8,4096,512]{2,1,0:T(8,128)(2,1)} async-done(((bf16[8,4096,128]{2,1,0:T(8,128)(2,1)}), bf16[8,4096,512]{2,1,0:T(8,128)(2,1)}) %all-gather.2.cloned.1.call-update) | async-done | bytes 33554448 | tf_op jit(solution)/shard_map/all_gather | solution.py:14
  308.9 21.1 %fusion.5 = f32[8,256,512]{2,1,0:T(8,128)} fusion(bf16[8,4096,256]{2,1,0:T(8,128)(2,1)} %param.4, bf16[8,4096,512]{2,1,0:T(8,128)(2,1)} %all-gather.2.cloned.1.call-done), kind=kOutput, calls=%fused_computation.7 | convolution fusion | flops 8589934592 | bytes 54525952 | tf_op jit(solution)/shard_map/dar,dap->drp/dot_general | solution.py:15
  329.9 0.0 all-reduce.3.cloned.1.call-update
  330.0 0.0 reduce-scatter.2.cloned.1.call-start
  330.0 0.0 copy-done
  330.0 21.5 %fusion = f32[8,128,512]{1,2,0:T(8,128)} fusion(bf16[8,4096,512]{2,1,0:T(8,128)(2,1)} %all-gather.2.cloned.1.call-done, bf16[8,4096,128]{2,1,0:T(8,128)(2,1)} %param.5, f32[8,4096]{1,0:T(8,128)S(1)} %copy-done), kind=kOutput, calls=%fused_computation.1 | convolution fusion | flops 4307550208 | bytes 44171264 | tf_op jit(solution)/shard_map/dak,dap->dkp/dot_general | solution.py:18
  351.5 0.0 reduce-scatter.2.cloned.1.call-update
  351.5 75.1 %all-reduce.3.cloned.1.call-done = f32[8,256,512]{2,1,0:T(8,128)} async-done(((f32[8,256,512]{2,1,0:T(8,128)}), f32[8,256,512]{2,1,0:T(8,128)}) %all-reduce.3.cloned.1.call-update) | async-done | bytes 4194320 | tf_op jit(solution)/shard_map/psum | solution.py:22
  426.6 5.5 copy.9
  432.1 5.0 all-to-all-start
  437.1 0.2 all-reduce.5.cloned.1.call-start
  437.3 10.4 %fusion.2 = f32[8,64,1024]{2,1,0:T(8,128)} fusion(f32[8,256,1024]{2,1,0:T(8,128)} %param.7, f32[8,256,512]{2,1,0:T(8,128)} %all-reduce.3.cloned.1.call-done, s32[]{:T(128)S(6)} %select_n.3), kind=kOutput, calls=%fused_computation.4 | convolution fusion | flops 1610612736 | bytes 11534340 | tf_op jit(solution)/shard_map/dri,drs->dis/dot_general | solution.py:27
  447.7 0.0 all-reduce.5.cloned.1.call-update
  447.7 47.9 %all-to-all-done = f32[8,256,512]{1,0,2:T(8,128)} async-done(((f32[8,256,512]{1,0,2:T(8,128)}), f32[8,256,512]{1,0,2:T(8,128)}, u32[]{:S(2)}, u32[]{:S(2)}) %all-to-all-start) | async-done | bytes 4194336 | tf_op jit(solution)/shard_map/all_to_all | solution.py:31
  495.6 5.3 copy.10
  500.9 0.0 reduce-scatter.2.cloned.1.call-done
  500.9 44.7 %all-reduce.5.cloned.1.call-done = f32[8,64,1024]{2,1,0:T(8,128)} async-done(((f32[8,64,1024]{2,1,0:T(8,128)}), f32[8,64,1024]{2,1,0:T(8,128)}) %all-reduce.5.cloned.1.call-update) | async-done | bytes 2097168 | tf_op jit(solution)/shard_map/psum | solution.py:30
  545.7 6.2 %convolution_add_fusion = f32[8,64,128]{2,1,0:T(8,128)} fusion(f32[8,64,1024]{2,1,0:T(8,128)} %all-reduce.5.cloned.1.call-done, f32[8,1024,128]{2,1,0:T(8,128)} %bitcast.12, f32[8,128,64]{1,2,0:T(8,128)} %reduce-scatter.2.cloned.1.call-done), kind=kOutput, calls=%fused_computation.3 | convolution fusion | flops 805371904 | bytes 6815744 | tf_op jit(solution)/shard_map/dir,drk->dik/dot_general | solution.py:32
Async XLA Ops:
  6.5 302.3 %all-gather.2.cloned.1.call-start = ((), (), s32[]{:S(2)}) async-start(), calls=%async_computation.2 | async-start | bytes 41943040 | tf_op jit(solution)/shard_map/all_gather | solution.py:14
  7.3 322.8 %copy-start = (f32[8,4096]{1,0:T(8,128)S(1)}, f32[8,4096]{1,0:T(8,128)}, u32[]{:S(2)}) copy-start(f32[8,4096]{1,0:T(8,128)} %param.6) | copy-start | bytes 393220
  7.3 419.3 %all-reduce.3.cloned.1.call-start = ((), (), s32[]{:S(2)}) async-start(), calls=%async_computation.3 | async-start | bytes 8388608 | tf_op jit(solution)/shard_map/psum | solution.py:22
  330.0 171.0 %reduce-scatter.2.cloned.1.call-start = ((), (), s32[]{:S(2)}) async-start(), calls=%async_computation.5 | async-start | bytes 2359296 | tf_op jit(solution)/shard_map/reduce_scatter | solution.py:23
  432.1 63.5 %all-to-all-start = ((f32[8,256,512]{1,0,2:T(8,128)}), f32[8,256,512]{1,0,2:T(8,128)}, u32[]{:S(2)}, u32[]{:S(2)}) async-start(f32[8,256,512]{1,0,2:T(8,128)} %copy.9), calls=%async_computation | async-start | bytes 8388608 | tf_op jit(solution)/shard_map/all_to_all | solution.py:31
  437.1 108.6 %all-reduce.5.cloned.1.call-start = ((), (), s32[]{:S(2)}) async-start(), calls=%async_computation.4 | async-start | bytes 4194304 | tf_op jit(solution)/shard_map/psum | solution.py:30
Sparse Core Ops, SparseCore 0:
  9.2 299.6 all-gather.1
  330.1 96.4 all-reduce.2
  428.9 36.0 reduce-scatter.1
  468.0 77.6 all-reduce.4
where the time goes:
time: 559 us; the launch traced here: 558 us
  waiting for transfers between devices  470 us (84%)
  matrix products  59.1 us (11%)
  between operations  13.2 us (2%)
  local copies, waits for them, and re-layouts  10.8 us (2%)
    all_gather x1, waiting for transfers between devices, shards(): fragment = lax.all_gather(weights, 'col', axis=2, tiled=True)  302 us
    psum x1, waiting for transfers between devices, shards(): exposure = lax.psum(joined[:, :factor_cols, :], 'row')  75.1 us
    all_to_all x1, waiting for transfers between devices, shards(): lax.all_to_all(exposure, 'col', split_axis=2, concat_axis=1, tiled=True)  47.9 us
    psum x1, waiting for transfers between devices, shards(): left = lax.psum(left_part, 'col')  44.7 us
    dot_general x1, matrix products, shards(): jnp.einsum('dak,dap->dkp', weighted, fragment, preferred_element_type=jnp...  21.5 us
    dot_general x1, matrix products, shards(): jnp.einsum('dar,dap->drp', loadings, fragment, preferred_element_type=jnp...  21.1 us
  transfers between devices with their start and end apart: 5, of which 4 were waited for; matrix products, arithmetic and copies ran while one was open for 8% of the time, Pallas kernels for 0%

commit v1 on v0

--- a/solution.py
+++ b/solution.py
@@ -27,7 +27,7 @@
     left_part = jnp.einsum(
         "dri,drs->dis", exposure_rows, factor_cov, precision=lax.Precision.HIGHEST
     )
-    left = lax.psum(left_part, "col")
+    left = jnp.sum(lax.all_gather(left_part, "col"), axis=0)
     exposure_cols = lax.all_to_all(exposure, "col", split_axis=2, concat_axis=1, tiled=True)
     factor_block = jnp.einsum("dir,drk->dik", left, exposure_cols, precision=lax.Precision.HIGHEST)
     return factor_block + jnp.swapaxes(specific_block, 1, 2)

time: 559 us -> 614 us (1.098)
  blocking collectives: 0 us -> 93.3 us
  waiting for transfers between devices: 470 us -> 432 us
    all_to_all x0 -> x1, blocking collectives: none -> 93.3 us  [shards(): lax.all_to_all(exposure, 'col', split_axis=2, concat_axis=1, tiled=True)]
    all_to_all x1 -> x0, waiting for transfers between devices: 47.9 us -> none  [shards(): lax.all_to_all(exposure, 'col', split_axis=2, concat_axis=1, tiled=True)]
    psum x1 -> x0, waiting for transfers between devices: 44.7 us -> none  [shards(): left = lax.psum(left_part, 'col')]
    reduce_scatter x1, waiting for transfers between devices: 0.01 us -> 32.9 us  [shards(): lax.psum_scatter(joined[:, factor_cols:, :], 'row', scatter_dimension=2,...]
    psum x1, waiting for transfers between devices: 75.1 us -> 96.6 us  [shards(): exposure = lax.psum(joined[:, :factor_cols, :], 'row')]
  transfers between devices with their start and end apart: 5 -> 4, of which waited for: 4 -> 3; matrix products, arithmetic and copies ran while one was open for 8% -> 6% of each run, Pallas kernels for 0% -> 0%
where the time goes in v1:
time: 614 us; the launch traced here: 613 us
  waiting for transfers between devices  432 us (70%)
  blocking collectives  93.3 us (15%)
  matrix products  59.6 us (10%)
  between operations  13.2 us (2%)
  local copies, waits for them, and re-layouts  10.8 us (2%)
    all_gather x1, waiting for transfers between devices, shards(): fragment = lax.all_gather(weights, 'col', axis=2, tiled=True)  302 us
    psum x1, waiting for transfers between devices, shards(): exposure = lax.psum(joined[:, :factor_cols, :], 'row')  96.6 us
    all_to_all x1, blocking collectives, shards(): lax.all_to_all(exposure, 'col', split_axis=2, concat_axis=1, tiled=True)  93.3 us
    reduce_scatter x1, waiting for transfers between devices, shards(): lax.psum_scatter(joined[:, factor_cols:, :], 'row', scatter_dimension=2,...  32.9 us
    dot_general x1, matrix products, shards(): jnp.einsum('dak,dap->dkp', weighted, fragment, preferred_element_type=jnp...  22.5 us
    dot_general x1, matrix products, shards(): jnp.einsum('dar,dap->drp', loadings, fragment, preferred_element_type=jnp...  21.2 us
  transfers between devices with their start and end apart: 4, of which 3 were waited for; matrix products, arithmetic and copies ran while one was open for 6% of the time, Pallas kernels for 0%

profile of v1, /device:TPU:0, one launch (start us, length us, event | category | flops | bytes accessed | tf_op | source)
XLA Modules:
  0.0 613.5 jit_solution(17636186278484013295)
XLA Ops:
  6.5 0.0 all-gather.4.cloned.1.call-start
  6.5 0.7 all-gather.4.cloned.1.call-update
  7.3 0.0 all-reduce.2.cloned.1.call-start
  7.3 301.6 %all-gather.4.cloned.1.call-done = bf16[8,4096,512]{2,1,0:T(8,128)(2,1)} async-done(((bf16[8,4096,128]{2,1,0:T(8,128)(2,1)}), bf16[8,4096,512]{2,1,0:T(8,128)(2,1)}) %all-gather.4.cloned.1.call-update) | async-done | bytes 33554448 | tf_op jit(solution)/shard_map/all_gather | solution.py:14
  308.9 21.2 %fusion.5 = f32[8,256,512]{2,1,0:T(8,128)} fusion(bf16[8,4096,256]{2,1,0:T(8,128)(2,1)} %param.4, bf16[8,4096,512]{2,1,0:T(8,128)(2,1)} %all-gather.4.cloned.1.call-done), kind=kOutput, calls=%fused_computation.7 | convolution fusion | flops 8589934592 | bytes 54525952 | tf_op jit(solution)/shard_map/dar,dap->drp/dot_general | solution.py:15
  330.0 0.0 copy-start
  330.0 0.0 all-reduce.2.cloned.1.call-update
  330.1 0.0 all-gather.6.cloned.1.call-start
  330.1 96.6 %all-reduce.2.cloned.1.call-done = f32[8,256,512]{2,1,0:T(8,128)} async-done(((f32[8,256,512]{2,1,0:T(8,128)}), f32[8,256,512]{2,1,0:T(8,128)}) %all-reduce.2.cloned.1.call-update) | async-done | bytes 4194320 | tf_op jit(solution)/shard_map/psum | solution.py:22
  426.7 10.4 %fusion.2 = f32[8,64,1024]{2,1,0:T(8,128)} fusion(f32[8,256,1024]{2,1,0:T(8,128)} %param.7, f32[8,256,512]{2,1,0:T(8,128)} %all-reduce.2.cloned.1.call-done, s32[]{:T(128)S(6)} %select_n.3), kind=kOutput, calls=%fused_computation.4 | convolution fusion | flops 1610612736 | bytes 11534340 | tf_op jit(solution)/shard_map/dri,drs->dis/dot_general | solution.py:27
  437.2 0.0 all-gather.6.cloned.1.call-update
  437.2 0.2 reduce-scatter.2.cloned.1.call-start
  437.4 0.0 copy-done
  437.4 22.5 %fusion = f32[8,128,512]{1,2,0:T(8,128)} fusion(bf16[8,4096,512]{2,1,0:T(8,128)(2,1)} %all-gather.4.cloned.1.call-done, bf16[8,4096,128]{2,1,0:T(8,128)(2,1)} %param.5, f32[8,4096]{1,0:T(8,128)S(1)} %copy-done), kind=kOutput, calls=%fused_computation.1 | convolution fusion | flops 4307550208 | bytes 44171264 | tf_op jit(solution)/shard_map/dak,dap->dkp/dot_general | solution.py:18
  459.9 0.0 reduce-scatter.2.cloned.1.call-update
  459.9 5.4 copy.11
  465.4 93.3 %all_to_all.18 = f32[8,256,512]{1,0,2:T(8,128)} all-to-all(f32[8,256,512]{1,0,2:T(8,128)} %copy.11), channel_id=1, replica_groups=mesh['row'=8,'col'=4] {'col'}, dimensions={2} | all-to-all | bytes 8388608 | tf_op jit(solution)/shard_map/all_to_all | solution.py:31
  558.6 5.3 copy.12
  563.9 0.0 all-gather.6.cloned.1.call-done
  563.9 4.6 reduce_sum.9
  568.5 32.9 %reduce-scatter.2.cloned.1.call-done = f32[8,128,64]{1,2,0:T(8,128)} async-done(((f32[8,128,512]{1,2,0:T(8,128)}), f32[8,128,64]{1,2,0:T(8,128)}) %reduce-scatter.2.cloned.1.call-update) | async-done | bytes 262160 | tf_op jit(solution)/shard_map/reduce_scatter | solution.py:23
  601.4 5.5 convolution_add_fusion
Async XLA Ops:
  6.5 302.3 %all-gather.4.cloned.1.call-start = ((), (), s32[]{:S(2)}) async-start(), calls=%async_computation.2 | async-start | bytes 41943040 | tf_op jit(solution)/shard_map/all_gather | solution.py:14
  7.3 419.5 %all-reduce.2.cloned.1.call-start = ((), (), s32[]{:S(2)}) async-start(), calls=%async_computation.3 | async-start | bytes 8388608 | tf_op jit(solution)/shard_map/psum | solution.py:22
  330.0 107.4 %copy-start = (f32[8,4096]{1,0:T(8,128)S(1)}, f32[8,4096]{1,0:T(8,128)}, u32[]{:S(2)}) copy-start(f32[8,4096]{1,0:T(8,128)} %param.6) | copy-start | bytes 393220
  330.1 233.9 %all-gather.6.cloned.1.call-start = ((), (), s32[]{:S(2)}) async-start(), calls=%async_computation.5 | async-start | bytes 10485760 | tf_op jit(solution)/shard_map/all_gather | solution.py:30
  437.2 164.3 %reduce-scatter.2.cloned.1.call-start = ((), (), s32[]{:S(2)}) async-start(), calls=%async_computation.4 | async-start | bytes 2359296 | tf_op jit(solution)/shard_map/reduce_scatter | solution.py:23
Sparse Core Ops, SparseCore 0:
  9.2 299.6 all-gather.3
  330.2 96.4 all-reduce.1
  437.3 126.4 all-gather.5
  565.9 35.4 reduce-scatter.1

commit v2 on v0

--- a/solution.py
+++ b/solution.py
@@ -11,7 +11,7 @@
     port_rows = total_ports // lax.axis_size("row")
     row_start = lax.axis_index("row") * port_rows
     weighted = (specific[:, :, None] * weights.astype(jnp.float32)).astype(jnp.bfloat16)
-    fragment = lax.all_gather(weights, "col", axis=2, tiled=True)
+    fragment = jnp.concatenate(lax.all_gather(weights, "col"), axis=2)
     exposure_part = jnp.einsum(
         "dar,dap->drp", loadings, fragment, preferred_element_type=jnp.float32
     )

time: 559 us -> 673 us (1.20)
  local copies, waits for them, and re-layouts: 10.8 us -> 97.3 us
  blocking collectives: 0 us -> 70.4 us
  waiting for transfers between devices: 470 us -> 431 us
    all_to_all x0 -> x1, blocking collectives: none -> 70.4 us  [shards(): lax.all_to_all(exposure, 'col', split_axis=2, concat_axis=1, tiled=True)]
    reshape x0 -> x1, local copies, waits for them, and re-layouts: none -> 48.5 us  [shards(): fragment = jnp.concatenate(lax.all_gather(weights, 'col'), axis=2)]
    all_to_all x1 -> x0, waiting for transfers between devices: 47.9 us -> none  [shards(): lax.all_to_all(exposure, 'col', split_axis=2, concat_axis=1, tiled=True)]
    psum x1, waiting for transfers between devices: 44.7 us -> 0.01 us  [shards(): left = lax.psum(left_part, 'col')]
    all_gather x0 -> x1, local copies, waits for them, and re-layouts: none -> 38 us  [shards(): fragment = jnp.concatenate(lax.all_gather(weights, 'col'), axis=2)]
    reduce_scatter x1, waiting for transfers between devices: 0.01 us -> 31.7 us  [shards(): lax.psum_scatter(joined[:, factor_cols:, :], 'row', scatter_dimension=2,...]
    psum x1, waiting for transfers between devices: 75.1 us -> 96.6 us  [shards(): exposure = lax.psum(joined[:, :factor_cols, :], 'row')]
  transfers between devices with their start and end apart: 5 -> 4, of which waited for: 4 -> 3; matrix products, arithmetic and copies ran while one was open for 8% -> 5% of each run, Pallas kernels for 0% -> 0%
where the time goes in v2:
time: 673 us; the launch traced here: 671 us
  waiting for transfers between devices  431 us (64%)
  local copies, waits for them, and re-layouts  97.3 us (14%)
  blocking collectives  70.4 us (10%)
  matrix products  59 us (9%)
  between operations  13.1 us (2%)
    all_gather x1, waiting for transfers between devices, shards(): fragment = jnp.concatenate(lax.all_gather(weights, 'col'), axis=2)  302 us
    psum x1, waiting for transfers between devices, shards(): exposure = lax.psum(joined[:, :factor_cols, :], 'row')  96.6 us
    all_to_all x1, blocking collectives, shards(): lax.all_to_all(exposure, 'col', split_axis=2, concat_axis=1, tiled=True)  70.4 us
    reshape x1, local copies, waits for them, and re-layouts, shards(): fragment = jnp.concatenate(lax.all_gather(weights, 'col'), axis=2)  48.5 us
    all_gather x1, local copies, waits for them, and re-layouts, shards(): fragment = jnp.concatenate(lax.all_gather(weights, 'col'), axis=2)  38 us
    reduce_scatter x1, waiting for transfers between devices, shards(): lax.psum_scatter(joined[:, factor_cols:, :], 'row', scatter_dimension=2,...  31.7 us
    dot_general x1, matrix products, shards(): jnp.einsum('dak,dap->dkp', weighted, fragment, preferred_element_type=jnp...  21.4 us
    dot_general x1, matrix products, shards(): jnp.einsum('dar,dap->drp', loadings, fragment, preferred_element_type=jnp...  21.1 us
  transfers between devices with their start and end apart: 4, of which 3 were waited for; matrix products, arithmetic and copies ran while one was open for 5% of the time, Pallas kernels for 0%

profile of v2, /device:TPU:0, one launch (start us, length us, event | category | flops | bytes accessed | tf_op | source)
XLA Modules:
  0.0 671.0 jit_solution(3566894460127536789)
XLA Ops:
  6.5 0.0 all-gather.3.cloned.1.call-start
  6.5 0.7 all-gather.3.cloned.1.call-update
  7.3 0.0 all-reduce.3.cloned.1.call-start
  7.3 301.7 %all-gather.3.cloned.1.call-done = bf16[32,4096,128]{2,1,0:T(8,128)(2,1)} async-done(((bf16[8,4096,128]{2,1,0:T(8,128)(2,1)}), bf16[32,4096,128]{2,1,0:T(8,128)(2,1)}) %all-gather.3.cloned.1.call-update) | async-done | bytes 33554448 | tf_op jit(solution)/shard_map/all_gather | solution.py:14
  309.0 38.0 %copy.17 = bf16[4,8,4096,128]{3,0,2,1:T(4,128)(2,1)} copy(bf16[4,8,4096,128]{3,2,1,0:T(8,128)(2,1)} %bitcast.17) | data formatting | bytes 67108864 | tf_op jit(solution)/shard_map/all_gather | solution.py:14
  347.0 48.5 %reshape.8 = bf16[8,4096,512]{2,1,0:T(8,128)(2,1)} reshape(bf16[8,4096,4,128]{3,2,1,0:T(4,128)(2,1)} %bitcast.16) | data formatting | bytes 67108864 | tf_op jit(solution)/shard_map/reshape | solution.py:14
  395.5 21.1 %fusion.5 = f32[8,256,512]{2,1,0:T(8,128)} fusion(bf16[8,4096,256]{2,1,0:T(8,128)(2,1)} %param.4, bf16[8,4096,512]{2,1,0:T(8,128)(2,1)} %reshape.8), kind=kOutput, calls=%fused_computation.8 | convolution fusion | flops 8589934592 | bytes 54525952 | tf_op jit(solution)/shard_map/dar,dap->drp/dot_general | solution.py:15
  416.6 0.0 copy-start
  416.6 0.0 all-reduce.3.cloned.1.call-update
  416.6 0.0 all-reduce.5.cloned.1.call-start
  416.7 96.6 %all-reduce.3.cloned.1.call-done = f32[8,256,512]{2,1,0:T(8,128)} async-done(((f32[8,256,512]{2,1,0:T(8,128)}), f32[8,256,512]{2,1,0:T(8,128)}) %all-reduce.3.cloned.1.call-update) | async-done | bytes 4194320 | tf_op jit(solution)/shard_map/psum | solution.py:22
  513.3 10.4 %fusion.2 = f32[8,64,1024]{2,1,0:T(8,128)} fusion(f32[8,256,1024]{2,1,0:T(8,128)} %param.7, f32[8,256,512]{2,1,0:T(8,128)} %all-reduce.3.cloned.1.call-done, s32[]{:T(128)S(6)} %select_n.3), kind=kOutput, calls=%fused_computation.5 | convolution fusion | flops 1610612736 | bytes 11534340 | tf_op jit(solution)/shard_map/dri,drs->dis/dot_general | solution.py:27
  523.7 0.0 all-reduce.5.cloned.1.call-update
  523.7 0.2 reduce-scatter.2.cloned.1.call-start
  523.9 0.0 copy-done
  523.9 21.4 %fusion = f32[8,128,512]{1,2,0:T(8,128)} fusion(bf16[8,4096,512]{2,1,0:T(8,128)(2,1)} %reshape.8, bf16[8,4096,128]{2,1,0:T(8,128)(2,1)} %param.5, f32[8,4096]{1,0:T(8,128)S(1)} %copy-done), kind=kOutput, calls=%fused_computation.2 | convolution fusion | flops 4307550208 | bytes 44171264 | tf_op jit(solution)/shard_map/dak,dap->dkp/dot_general | solution.py:18
  545.3 0.0 reduce-scatter.2.cloned.1.call-update
  545.4 5.4 copy.11
  550.8 70.4 %all_to_all.18 = f32[8,256,512]{1,0,2:T(8,128)} all-to-all(f32[8,256,512]{1,0,2:T(8,128)} %copy.11), channel_id=1, replica_groups=mesh['row'=8,'col'=4] {'col'}, dimensions={2} | all-to-all | bytes 8388608 | tf_op jit(solution)/shard_map/all_to_all | solution.py:31
  621.2 5.3 copy.12
  626.6 0.0 all-reduce.5.cloned.1.call-done
  626.6 31.7 %reduce-scatter.2.cloned.1.call-done = f32[8,128,64]{1,2,0:T(8,128)} async-done(((f32[8,128,512]{1,2,0:T(8,128)}), f32[8,128,64]{1,2,0:T(8,128)}) %reduce-scatter.2.cloned.1.call-update) | async-done | bytes 262160 | tf_op jit(solution)/shard_map/reduce_scatter | solution.py:23
  658.2 6.2 convolution_add_fusion
Async XLA Ops:
  6.5 302.5 %all-gather.3.cloned.1.call-start = ((), (), s32[]{:S(2)}) async-start(), calls=%async_computation.5 | async-start | bytes 41943040 | tf_op jit(solution)/shard_map/all_gather | solution.py:14
  7.3 506.0 %all-reduce.3.cloned.1.call-start = ((), (), s32[]{:S(2)}) async-start(), calls=%async_computation.2 | async-start | bytes 8388608 | tf_op jit(solution)/shard_map/psum | solution.py:22
  416.6 107.3 %copy-start = (f32[8,4096]{1,0:T(8,128)S(1)}, f32[8,4096]{1,0:T(8,128)}, u32[]{:S(2)}) copy-start(f32[8,4096]{1,0:T(8,128)} %param.6) | copy-start | bytes 393220
  416.6 209.9 %all-reduce.5.cloned.1.call-start = ((), (), s32[]{:S(2)}) async-start(), calls=%async_computation.3 | async-start | bytes 4194304 | tf_op jit(solution)/shard_map/psum | solution.py:30
  523.7 134.5 %reduce-scatter.2.cloned.1.call-start = ((), (), s32[]{:S(2)}) async-start(), calls=%async_computation.4 | async-start | bytes 2359296 | tf_op jit(solution)/shard_map/reduce_scatter | solution.py:23
Sparse Core Ops, SparseCore 0:
  9.2 299.7 all-gather.2
  416.7 96.4 all-reduce.2
  523.8 96.3 all-reduce.4
  622.3 35.8 reduce-scatter.1
